TPU v7x, 1024 devices: a whole 8x8x8 slice. The times are simulated.
1024 devices in a mesh: gx: 32 (over y_hi, x), gy: 8 (over z), gz: 4 (over y_lo, core).
Axes of the slice: x: 8, y: 8 (y_hi: 4, y_lo: 2; y = y_hi * 2 + y_lo), z: 8, core: 2. Of those that a mesh axis runs over, the one named last changes fastest.
Arguments:
- displacement: float32 [32, 8, 18432], P('gx', 'gy', 'gz'), may hold values from -0.1 to 0.1
- species: int32 [32, 8, 6144], P('gx', 'gy', 'gz'), may hold values from 0 to 1
- centres: int32 [32, 8, 64], P('gx', 'gy', 'gz'), may hold values from 0 to 1535, as said below
- neighbours: int32 [32, 8, 2048], P('gx', 'gy', 'gz'), may hold values from 0 to 5183, as said below
- neighbour_count: int32 [32, 8, 64], P('gx', 'gy', 'gz'), may hold values from 1 to 32, as said below
- live_centres: int32 [32, 8, 4], P('gx', 'gy', 'gz'), may hold values from 8 to 16, as said below
- w_two: float32 [12, 64], replicated, may hold values from -1.75 to 1.75
- w_lat: float32 [64, 64], replicated, may hold values from -0.75 to 0.75
- w_env: float32 [64, 64], replicated, may hold values from -0.75 to 0.75
- w_out: float32 [256, 64], replicated, may hold values from -0.375 to 0.375
- readout: float32 [64], replicated, may hold values from -0.75 to 0.75
Outputs:
- centre_energy: float32 [32, 8, 64], P('gx', 'gy', 'gz')
- forces: float32 [32, 8, 18432], P('gx', 'gy', 'gz')
Inputs may be any that keep to these rules, and one draw needn't show every extreme that they name: `centres`: local atom index of an owned atom; entries may repeat. `neighbours`: extended index of an atom whose cell lies within two cells of the centre's cell in each dimension, with squared cell distance at most 4; never the centre itself. `neighbour_count`: in every domain some centre has all 32 slots live. `live_centres`: some domain has all 16 centres live; the live centres are the first ones.
All inputs are finite; a program needn't handle non-finite values.
Results may differ from a plain program's by a relative error of at most 0.0003.
Values sent between devices are 32-bit elements; how exact they have to be, the bound alone decides.
No kernel may reach another device: no remote copies, remote signals or barrier semaphores. Data moves between devices by JAX's collectives and lax.ppermute only.
A program may use at most 32 MiB of HBM per device.

v0:
```python
import math

import jax
import jax.numpy as jnp
import numpy as np
from jax import lax
from jax.sharding import PartitionSpec as P

CELLS = 8
NBASIS = 8
SPECIES = 2


cutoff = 6.0
cell_side = 3.1
env_scale = 0.2
block_limit = 64
site_rows = np.array([[0.25, 0.25, 0.25], [0.75, 0.75, 0.25], [0.25, 0.75, 0.75]], np.float32)


def shifted(shard, axis, by):
    length = lax.axis_size(axis)
    return lax.ppermute(shard, axis, [(i, (i + by) % length) for i in range(length)])


def with_halo(shard, sides, width):
    for axis, dim in sides:
        size, length = (lax.axis_size(axis), shard.shape[dim])
        up = [(i, (i + 1) % size) for i in range(size)]
        down = [(j, i) for i, j in up]
        last = lax.slice_in_dim(shard, length - width, length, axis=dim)
        first = lax.slice_in_dim(shard, 0, width, axis=dim)
        before = lax.ppermute(last, axis, up)
        after = lax.ppermute(first, axis, down)
        shard = jnp.concatenate([before, shard, after], axis=dim)
    return shard


def mixing(weight, data):
    return jnp.dot(
        weight.T, data, precision=lax.Precision.HIGHEST, preferred_element_type=jnp.float32
    )


def harmonics(unit):
    ux, uy, uz = (unit[0], unit[1], unit[2])
    root3 = math.sqrt(3.0)
    root5 = math.sqrt(5.0)
    root15 = math.sqrt(15.0)
    return jnp.stack(
        [
            jnp.ones_like(ux),
            root3 * ux,
            root3 * uy,
            root3 * uz,
            root15 * ux * uy,
            root15 * uy * uz,
            0.5 * root5 * (3.0 * uz * uz - 1.0),
            root15 * ux * uz,
            0.5 * root15 * (ux * ux - uy * uy),
        ],
        0,
    )


def block_energy(rvec, kind_first, kind_second, live, w_two, w_lat, w_env, w_out, readout, slots):
    dist = jnp.sqrt(jnp.sum(rvec * rvec, axis=0))
    unit = rvec / dist
    ratio = dist / cutoff
    envelope = jnp.where(
        ratio < 1.0, 1.0 - 28.0 * ratio**6 + 48.0 * ratio**7 - 21.0 * ratio**8, 0.0
    )
    orders = jnp.arange(1, NBASIS + 1, dtype=jnp.float32)[:, None]
    basis = (
        math.sqrt(2.0 / cutoff)
        * jnp.sin(orders * math.pi * dist[None, :] / cutoff)
        / dist[None, :]
        * envelope[None, :]
    )
    kinds = jnp.arange(SPECIES, dtype=jnp.float32)[:, None]
    first_hot = (kind_first[None, :] == kinds).astype(jnp.float32)
    second_hot = (kind_second[None, :] == kinds).astype(jnp.float32)
    inputs = jnp.concatenate([first_hot, second_hot, basis], 0)
    hidden = jax.nn.silu(mixing(w_two, inputs))
    latent = jax.nn.silu(mixing(w_lat, hidden))
    weights = mixing(w_env, latent) * (envelope * live)[None, :]
    harm = harmonics(unit)
    width = latent.shape[0]
    centre_total = rvec.shape[1] // slots
    edge = (harm[:, None, :] * weights[None, :, :]).reshape(9, width, centre_total, slots)
    environ = env_scale * jnp.sum(edge, axis=3)
    product = edge * environ[:, :, :, None]
    scalars = jnp.stack(
        [product[0], jnp.sum(product[1:4], axis=0), jnp.sum(product[4:9], axis=0)], 0
    )
    joined = jnp.concatenate([latent, scalars.reshape(3 * width, centre_total * slots)], 0)
    updated = jax.nn.silu(mixing(w_out, joined))
    pair_energy = jnp.dot(readout, updated, precision=lax.Precision.HIGHEST) * envelope * live
    return jnp.sum(pair_energy.reshape(centre_total, slots), axis=1)


def along_gx(values, by):
    return shifted(values, "gx", by)


def along_gy(values, by):
    return shifted(values, "gy", by)


def along_gz(values, by):
    return shifted(values, "gz", by)


def fold_layers(values, axis_dim, mover):
    length = values.shape[axis_dim]
    inner_len = length - 4
    from_above = mover(lax.slice_in_dim(values, 0, 2, axis=axis_dim), -1)
    from_below = mover(lax.slice_in_dim(values, length - 2, length, axis=axis_dim), 1)
    inner = lax.slice_in_dim(values, 2, length - 2, axis=axis_dim)
    widths_low = [(0, 0)] * values.ndim
    widths_high = [(0, 0)] * values.ndim
    widths_low[axis_dim] = (0, inner_len - 2)
    widths_high[axis_dim] = (inner_len - 2, 0)
    return inner + jnp.pad(from_below, widths_low) + jnp.pad(from_above, widths_high)


def local(
    displacement,
    species,
    centres,
    neighbours,
    neighbour_count,
    live_centres,
    w_two,
    w_lat,
    w_env,
    w_out,
    readout,
):
    side_x = CELLS
    side_y = CELLS
    side_z = CELLS
    cells = jnp.concatenate(
        [
            displacement.reshape(side_x, side_y, side_z, 9),
            species.reshape(side_x, side_y, side_z, 3).astype(jnp.float32),
        ],
        axis=3,
    )
    padded = with_halo(cells, (("gx", 0), ("gy", 1), ("gz", 2)), 2)
    ext_x, ext_y, ext_z = (side_x + 4, side_y + 4, side_z + 4)
    total_ext = ext_x * ext_y * ext_z * 3
    shifts = padded[..., :9].reshape(ext_x, ext_y, ext_z, 3, 3)
    kinds = padded[..., 9:].reshape(1, total_ext)
    grid_x = jnp.arange(ext_x, dtype=jnp.float32)[:, None, None] - 2.0
    grid_y = jnp.arange(ext_y, dtype=jnp.float32)[None, :, None] - 2.0
    grid_z = jnp.arange(ext_z, dtype=jnp.float32)[None, None, :] - 2.0
    corner = jnp.stack(jnp.broadcast_arrays(grid_x, grid_y, grid_z), -1)
    sites = jnp.array(site_rows, dtype=jnp.float32)
    places = (corner[:, :, :, None, :] + sites[None, None, None, :, :] + shifts) * cell_side
    table = jnp.concatenate([places.reshape(total_ext, 3).T, kinds], 0)
    centre_list = centres.reshape(-1)
    centre_total = centre_list.shape[0]
    neighbour_list = neighbours.reshape(-1)
    slots = neighbour_list.shape[0] // centre_total
    count_list = neighbour_count.reshape(-1)
    alive = live_centres.reshape(())
    atom_first = centre_list % 3
    cell_first = centre_list // 3
    loc_z = cell_first % side_z
    loc_y = cell_first // side_z % side_y
    loc_x = cell_first // (side_z * side_y)
    first_ext = (((loc_x + 2) * ext_y + loc_y + 2) * ext_z + loc_z + 2) * 3 + atom_first
    slot_ids = jnp.arange(slots, dtype=jnp.int32)
    block_centres = min(block_limit, centre_total)

    def one_block(block, carry):
        forces, energies = carry
        start = block * block_centres
        first = jnp.repeat(first_ext, slots)
        rows_first = jnp.take(table, first, axis=1)
        rows_second = jnp.take(table, neighbour_list, axis=1)
        rvec = rows_second[:3] - rows_first[:3]
        centre_ids = start + jnp.arange(block_centres, dtype=jnp.int32)
        live = (
            ((slot_ids[None, :] < count_list[:, None]) & (centre_ids[:, None] < alive))
            .reshape(-1)
            .astype(jnp.float32)
        )

        def energy_of(vectors):
            return block_energy(
                vectors,
                rows_first[3],
                rows_second[3],
                live,
                w_two,
                w_lat,
                w_env,
                w_out,
                readout,
                slots,
            )

        energy, pullback = jax.vjp(energy_of, rvec)
        grad = pullback(jnp.ones_like(energy))[0]
        forces = forces.at[:, neighbour_list].add(-grad)
        forces = forces.at[:, first].add(grad)
        energies = lax.dynamic_update_slice_in_dim(energies, energy, start, 0)
        return (forces, energies)

    initial = (jnp.zeros((3, total_ext), jnp.float32), jnp.zeros((centre_total,), jnp.float32))
    block_total = centre_total // block_centres
    forces, energies = lax.fori_loop(0, block_total, one_block, initial)
    grid_forces = jnp.transpose(forces.reshape(3, ext_x, ext_y, ext_z, 3), (1, 2, 3, 4, 0)).reshape(
        ext_x, ext_y, ext_z, 9
    )
    owned = fold_layers(
        fold_layers(fold_layers(grid_forces, 0, along_gx), 1, along_gy), 2, along_gz
    )
    return (energies.reshape(1, 1, centre_total), owned.reshape(1, 1, side_x * side_y * side_z * 9))


def solution(mesh):
    in_specs = (
        P("gx", "gy", "gz"),
        P("gx", "gy", "gz"),
        P("gx", "gy", "gz"),
        P("gx", "gy", "gz"),
        P("gx", "gy", "gz"),
        P("gx", "gy", "gz"),
        P(),
        P(),
        P(),
        P(),
        P(),
    )
    out_specs = (P("gx", "gy", "gz"), P("gx", "gy", "gz"))
    return jax.shard_map(local, mesh=mesh, in_specs=in_specs, out_specs=out_specs, check_vma=False)
```

profile of v0, /device:TPU:46, one launch (start us, length us, event | category | flops | bytes accessed | tf_op | source)
XLA Modules:
  0.0 126.7 jit_solution(9324421357431388520)
XLA Ops:
  2.7 5.7 %collective-permute-start = (f32[2,8,8,12]{3,2,1,0:T(8,128)S(1)}, f32[2,8,8,12]{3,2,1,0:T(8,128)S(1)}, u32[]{:S(2)}, u32[]{:S(2)}) collective-permute-start(f32[2,8,8,12]{3,2,1,0:T(8,128)S(1)} %get-tuple-element.68), channel_id=1, source_target_pairs={{0,32},{32,64},{64,96},{96,128},{128,160},{160,192},{192,224},{224... | collective-permute-start | bytes 18440 | tf_op jit(solution)/shard_map/ppermute | solution.py:33
  8.5 1.9 %collective-permute-start.1 = (f32[2,8,8,12]{3,2,1,0:T(8,128)S(1)}, f32[2,8,8,12]{3,2,1,0:T(8,128)S(1)}, u32[]{:S(2)}, u32[]{:S(2)}) collective-permute-start(f32[2,8,8,12]{3,2,1,0:T(8,128)S(1)} %get-tuple-element.69), channel_id=1, source_target_pairs={{32,0},{64,32},{96,64},{128,96},{160,128},{192,160},{224,192},{256... | collective-permute-start | bytes 18440 | tf_op jit(solution)/shard_map/ppermute | solution.py:34
  14.3 3.0 %broadcast_add_fusion = f32[12,12,12,3,3]{3,2,1,0,4:T(8,128)} fusion(f32[3,3]{0,1:T(4,128)} %constant.170.clone, f32[12,12,12,3]{2,1,0,3:T(8,128)S(1)} %pad_maximum_fusion.2), kind=kLoop, calls=%fused_computation.12 | loop fusion | flops 15552 | bytes 82980 | tf_op jit(solution)/shard_map/add | solution.py:160
  17.4 1.9 %collective-permute-done.1 = f32[2,8,8,12]{3,2,1,0:T(8,128)S(1)} collective-permute-done((f32[2,8,8,12]{3,2,1,0:T(8,128)S(1)}, f32[2,8,8,12]{3,2,1,0:T(8,128)S(1)}, u32[]{:S(2)}, u32[]{:S(2)}) %collective-permute-start.1) | collective-permute-done | bytes 6176 | tf_op jit(solution)/shard_map/ppermute | solution.py:34
  19.4 5.2 %collective-permute-start.2 = (f32[12,2,8,12]{3,2,1,0:T(8,128)S(1)}, f32[12,2,8,12]{3,2,1,0:T(8,128)S(1)}, u32[]{:S(2)}, u32[]{:S(2)}) collective-permute-start(f32[12,2,8,12]{3,2,1,0:T(8,128)S(1)} %get-tuple-element.63), channel_id=1, source_target_pairs={{0,4},{4,8},{8,12},{12,16},{16,20},{20,24},{24,28},{28,0},{1,5},{5... | collective-permute-start | bytes 27656 | tf_op jit(solution)/shard_map/ppermute | solution.py:33
  24.6 14.8 %collective-permute-start.3 = (f32[12,2,8,12]{3,2,1,0:T(8,128)S(1)}, f32[12,2,8,12]{3,2,1,0:T(8,128)S(1)}, u32[]{:S(2)}, u32[]{:S(2)}) collective-permute-start(f32[12,2,8,12]{3,2,1,0:T(8,128)S(1)} %get-tuple-element.64), channel_id=1, source_target_pairs={{4,0},{8,4},{12,8},{16,12},{20,16},{24,20},{28,24},{0,28},{5,1},{9... | collective-permute-start | bytes 27656 | tf_op jit(solution)/shard_map/ppermute | solution.py:34
  40.1 1.5 %collective-permute-done.3 = f32[12,2,8,12]{3,2,1,0:T(8,128)S(1)} collective-permute-done((f32[12,2,8,12]{3,2,1,0:T(8,128)S(1)}, f32[12,2,8,12]{3,2,1,0:T(8,128)S(1)}, u32[]{:S(2)}, u32[]{:S(2)}) %collective-permute-start.3) | collective-permute-done | bytes 9248 | tf_op jit(solution)/shard_map/ppermute | solution.py:34
  41.8 1.9 %collective-permute-start.4 = (f32[12,12,2,12]{3,2,1,0:T(2,128)S(1)}, f32[12,12,2,12]{3,2,1,0:T(2,128)S(1)}, u32[]{:S(2)}, u32[]{:S(2)}) collective-permute-start(f32[12,12,2,12]{3,2,1,0:T(2,128)S(1)} %get-tuple-element.61), channel_id=1, source_target_pairs={{0,1},{1,2},{2,3},{3,0},{4,5},{5,6},{6,7},{7,4},{8,9},{9,10},{10,1... | collective-permute-start | bytes 41480 | tf_op jit(solution)/shard_map/ppermute | solution.py:33
  43.8 3.6 %collective-permute-start.5 = (f32[12,12,2,12]{3,2,1,0:T(2,128)S(1)}, f32[12,12,2,12]{3,2,1,0:T(2,128)S(1)}, u32[]{:S(2)}, u32[]{:S(2)}) collective-permute-start(f32[12,12,2,12]{3,2,1,0:T(2,128)S(1)} %get-tuple-element.62), channel_id=1, source_target_pairs={{1,0},{2,1},{3,2},{0,3},{5,4},{6,5},{7,6},{4,7},{9,8},{10,9},{11,1... | collective-permute-start | bytes 41480 | tf_op jit(solution)/shard_map/ppermute | solution.py:34
  47.4 3.3 %add.194 = f32[5184,3]{0,1:T(4,128)S(1)} reshape(f32[12,12,12,3,3]{3,2,1,0,4:T(8,128)} %broadcast_add_fusion) | data formatting | bytes 124416 | tf_op jit(solution)/shard_map/add | solution.py:160
  51.2 1.4 %slice.152 = f32[12,12,12,3]{3,2,1,0:T(8,128)} slice(f32[12,12,12,12]{3,2,1,0:T(8,128)S(1)} %pad_maximum_fusion), slice={[0:12], [0:12], [0:12], [9:12]} | slice | bytes 41472 | tf_op jit(solution)/shard_map/slice | solution.py:154
  52.7 2.0 %reshape.344 = f32[5184,3]{1,0:T(8,128)S(1)} reshape(f32[12,12,12,9]{3,2,1,0:T(8,128)} %bitcast.94) | data formatting | bytes 124416 | tf_op jit(solution)/shard_map/reshape | solution.py:153
  55.5 1.8 %reshape.345 = f32[1,5184]{1,0:T(1,128)S(1)} reshape(f32[12,12,12,3]{3,2,1,0:T(8,128)} %slice.152) | data formatting | bytes 41472 | tf_op jit(solution)/shard_map/reshape | solution.py:154
  58.2 1.0 gather_fusion
  59.3 1.0 gather_fusion.1
  68.6 1.6 %multiply_reduce_fusion.1 = (f32[64,16,32]{0,2,1:T(8,128)S(1)}, f32[9,16,32]{2,1,0:T(8,128)S(1)}) fusion(f32[1,64,16,32]{1,3,2,0:T(8,128)S(1)} %bitcast.100, f32[3,64,16,32]{1,3,2,0:T(8,128)S(1)} %broadcast_in_dim.80, f32[5,64,16,32]{1,3,2,0:T(8,128)S(1)} %broadcast_in_dim.79, f32[9,64,16]{1,2,0:T(8,128)S(1)} %broadcast_multiply_fusion.1, ...), kind=kLoop, calls=%fused_computation.8 | loop fusion | flops 2321920 | bytes 1552384 | tf_op jit(solution)/shard_map/while/body/eval_jaxpr/transpose(jvp())/reduce_sum | solution.py:90
  72.4 3.1 %scatter_custom_fusion = f32[3,5184]{0,1:T(8,128)S(1)} fusion(s32[512]{0:T(512)S(1)} %bitcast.115, f32[512,3]{1,0:T(8,128)S(1)} %copy.179, f32[]{:T(128)} %constant.151.clone.1), kind=kCustom, calls=%fused_computation.13 | custom fusion | flops 1536 | bytes 62212 | tf_op jit(solution)/shard_map/while/body/eval_jaxpr/scatter-add | solution.py:207
  75.5 5.0 %scatter_fusion = f32[3,5184]{0,1:T(8,128)S(1)} fusion(f32[3,5184]{0,1:T(8,128)S(1)} %scatter_custom_fusion, s32[512]{0:T(512)S(1)} %bitcast.112, f32[512,3]{1,0:T(8,128)S(1)} %copy.180), kind=kCustom, calls=%fused_computation.3 | custom fusion | flops 1536 | bytes 20480 | tf_op jit(solution)/shard_map/while/body/eval_jaxpr/scatter-add | solution.py:208
  81.3 3.1 %reshape.353 = f32[3,12,12,12,3]{4,3,2,1,0:T(8,128)} reshape(f32[3,5184]{1,0:T(4,128)S(1)} %copy.181) | data formatting | bytes 124416 | tf_op jit(solution)/shard_map/reshape | solution.py:215
  84.4 1.4 %fusion.83 = (f32[2,12,12,3,3]{3,2,1,0,4:T(8,128)S(1)}, f32[2,12,12,3,3]{3,2,1,0,4:T(8,128)S(1)}) fusion(f32[12,12,12,3,3]{3,2,1,0,4:T(8,128)} %bitcast.92), kind=kLoop, calls=%fused_computation.199 | loop fusion | bytes 41472 | tf_op jit(solution)/shard_map/slice | solution.py:118
  86.4 6.5 %collective-permute-start.6 = (f32[2,12,12,9]{2,0,3,1:T(2,128)S(1)}, f32[2,12,12,9]{2,0,3,1:T(2,128)S(1)}, u32[]{:S(2)}, u32[]{:S(2)}) collective-permute-start(f32[2,12,12,9]{2,0,3,1:T(2,128)S(1)} %bitcast.107), channel_id=1, source_target_pairs={{0,32},{32,64},{64,96},{96,128},{128,160},{160,192},{192,224},{224... | collective-permute-start | bytes 31112 | tf_op jit(solution)/shard_map/ppermute | solution.py:23
  93.5 1.9 %collective-permute-start.7 = (f32[2,12,12,9]{2,0,3,1:T(2,128)S(1)}, f32[2,12,12,9]{2,0,3,1:T(2,128)S(1)}, u32[]{:S(2)}, u32[]{:S(2)}) collective-permute-start(f32[2,12,12,9]{2,0,3,1:T(2,128)S(1)} %bitcast.108), channel_id=1, source_target_pairs={{0,992},{32,0},{64,32},{96,64},{128,96},{160,128},{192,160},{224,1... | collective-permute-start | bytes 31112 | tf_op jit(solution)/shard_map/ppermute | solution.py:23
  95.4 1.9 %slice.163 = f32[8,12,12,3,3]{3,2,1,0,4:T(8,128)S(1)} slice(f32[12,12,12,3,3]{3,2,1,0,4:T(8,128)} %bitcast.93), slice={[2:10], [0:12], [0:12], [0:3], [0:3]} | slice | bytes 82944 | tf_op jit(solution)/shard_map/slice | solution.py:119
  97.3 1.8 %copy.182 = f32[8,12,12,3,3]{2,0,4,3,1:T(8,128)S(1)} copy(f32[8,12,12,3,3]{3,2,1,0,4:T(8,128)S(1)} %slice.163) | data formatting | bytes 82944 | tf_op jit(solution)/shard_map/slice | solution.py:119
  99.1 6.5 %collective-permute-done.7 = f32[2,12,12,9]{2,0,3,1:T(2,128)S(1)} collective-permute-done((f32[2,12,12,9]{2,0,3,1:T(2,128)S(1)}, f32[2,12,12,9]{2,0,3,1:T(2,128)S(1)}, u32[]{:S(2)}, u32[]{:S(2)}) %collective-permute-start.7) | collective-permute-done | bytes 10400 | tf_op jit(solution)/shard_map/ppermute | solution.py:23
  105.8 1.9 %collective-permute-start.8 = (f32[8,2,12,9]{2,0,3,1:T(8,128)S(1)}, f32[8,2,12,9]{2,0,3,1:T(8,128)S(1)}, u32[]{:S(2)}, u32[]{:S(2)}) collective-permute-start(f32[8,2,12,9]{2,0,3,1:T(8,128)S(1)} %get-tuple-element.70), channel_id=1, source_target_pairs={{0,4},{4,8},{8,12},{12,16},{16,20},{20,24},{24,28},{28,0},{1,5},{5... | collective-permute-start | bytes 20744 | tf_op jit(solution)/shard_map/ppermute | solution.py:23
  107.7 5.5 %collective-permute-start.9 = (f32[8,2,12,9]{2,0,3,1:T(8,128)S(1)}, f32[8,2,12,9]{2,0,3,1:T(8,128)S(1)}, u32[]{:S(2)}, u32[]{:S(2)}) collective-permute-start(f32[8,2,12,9]{2,0,3,1:T(8,128)S(1)} %get-tuple-element.71), channel_id=1, source_target_pairs={{0,28},{4,0},{8,4},{12,8},{16,12},{20,16},{24,20},{28,24},{1,29},{... | collective-permute-start | bytes 20744 | tf_op jit(solution)/shard_map/ppermute | solution.py:23
  113.6 1.6 %collective-permute-done.9 = f32[8,2,12,9]{2,0,3,1:T(8,128)S(1)} collective-permute-done((f32[8,2,12,9]{2,0,3,1:T(8,128)S(1)}, f32[8,2,12,9]{2,0,3,1:T(8,128)S(1)}, u32[]{:S(2)}, u32[]{:S(2)}) %collective-permute-start.9) | collective-permute-done | bytes 6944 | tf_op jit(solution)/shard_map/ppermute | solution.py:23
  115.4 1.9 %collective-permute-start.10 = (f32[8,8,2,9]{2,0,3,1:T(8,128)S(1)}, f32[8,8,2,9]{2,0,3,1:T(8,128)S(1)}, u32[]{:S(2)}, u32[]{:S(2)}) collective-permute-start(f32[8,8,2,9]{2,0,3,1:T(8,128)S(1)} %get-tuple-element.72), channel_id=1, source_target_pairs={{0,1},{1,2},{2,3},{3,0},{4,5},{5,6},{6,7},{7,4},{8,9},{9,10},{10,1... | collective-permute-start | bytes 13832 | tf_op jit(solution)/shard_map/ppermute | solution.py:23
  117.3 3.6 %collective-permute-start.11 = (f32[8,8,2,9]{2,0,3,1:T(8,128)S(1)}, f32[8,8,2,9]{2,0,3,1:T(8,128)S(1)}, u32[]{:S(2)}, u32[]{:S(2)}) collective-permute-start(f32[8,8,2,9]{2,0,3,1:T(8,128)S(1)} %get-tuple-element.73), channel_id=1, source_target_pairs={{0,3},{1,0},{2,1},{3,2},{4,7},{5,4},{6,5},{7,6},{8,11},{9,8},{10,9... | collective-permute-start | bytes 13832 | tf_op jit(solution)/shard_map/ppermute | solution.py:23
  121.7 2.0 %collective-permute-done.10 = f32[8,8,2,9]{2,0,3,1:T(8,128)S(1)} collective-permute-done((f32[8,8,2,9]{2,0,3,1:T(8,128)S(1)}, f32[8,8,2,9]{2,0,3,1:T(8,128)S(1)}, u32[]{:S(2)}, u32[]{:S(2)}) %collective-permute-start.10) | collective-permute-done | bytes 4640 | tf_op jit(solution)/shard_map/ppermute | solution.py:23
  123.7 1.5 %collective-permute-done.11 = f32[8,8,2,9]{2,0,3,1:T(8,128)S(1)} collective-permute-done((f32[8,8,2,9]{2,0,3,1:T(8,128)S(1)}, f32[8,8,2,9]{2,0,3,1:T(8,128)S(1)}, u32[]{:S(2)}, u32[]{:S(2)}) %collective-permute-start.11) | collective-permute-done | bytes 4640 | tf_op jit(solution)/shard_map/ppermute | solution.py:23
  (126 shorter events, 23.4 us)
Async XLA Ops:
  0.6 64.7 %copy-start = (f32[256,64]{0,1:T(8,128)S(1)}, f32[256,64]{0,1:T(8,128)}, u32[]{:S(2)}) copy-start(f32[256,64]{0,1:T(8,128)} %param.23) | copy-start | bytes 196612
  2.7 14.6 %collective-permute-start = (f32[2,8,8,12]{3,2,1,0:T(8,128)S(1)}, f32[2,8,8,12]{3,2,1,0:T(8,128)S(1)}, u32[]{:S(2)}, u32[]{:S(2)}) collective-permute-start(f32[2,8,8,12]{3,2,1,0:T(8,128)S(1)} %get-tuple-element.68), channel_id=1, source_target_pairs={{0,32},{32,64},{64,96},{96,128},{128,160},{160,192},{192,224},{224... | collective-permute-start | bytes 18440 | tf_op jit(solution)/shard_map/ppermute | solution.py:33
  8.5 10.8 %collective-permute-start.1 = (f32[2,8,8,12]{3,2,1,0:T(8,128)S(1)}, f32[2,8,8,12]{3,2,1,0:T(8,128)S(1)}, u32[]{:S(2)}, u32[]{:S(2)}) collective-permute-start(f32[2,8,8,12]{3,2,1,0:T(8,128)S(1)} %get-tuple-element.69), channel_id=1, source_target_pairs={{32,0},{64,32},{96,64},{128,96},{160,128},{192,160},{224,192},{256... | collective-permute-start | bytes 18440 | tf_op jit(solution)/shard_map/ppermute | solution.py:34
  14.1 3.2 %copy-start.4 = (s32[1,1,16]{2,1,0:T(1,128)S(1)}, s32[1,1,16]{2,1,0:T(1,128)}, u32[]{:S(2)}) copy-start(s32[1,1,16]{2,1,0:T(1,128)} %param.18) | copy-start | bytes 196
  19.4 20.7 %collective-permute-start.2 = (f32[12,2,8,12]{3,2,1,0:T(8,128)S(1)}, f32[12,2,8,12]{3,2,1,0:T(8,128)S(1)}, u32[]{:S(2)}, u32[]{:S(2)}) collective-permute-start(f32[12,2,8,12]{3,2,1,0:T(8,128)S(1)} %get-tuple-element.63), channel_id=1, source_target_pairs={{0,4},{4,8},{8,12},{12,16},{16,20},{20,24},{24,28},{28,0},{1,5},{5... | collective-permute-start | bytes 27656 | tf_op jit(solution)/shard_map/ppermute | solution.py:33
  24.6 17.0 %collective-permute-start.3 = (f32[12,2,8,12]{3,2,1,0:T(8,128)S(1)}, f32[12,2,8,12]{3,2,1,0:T(8,128)S(1)}, u32[]{:S(2)}, u32[]{:S(2)}) collective-permute-start(f32[12,2,8,12]{3,2,1,0:T(8,128)S(1)} %get-tuple-element.64), channel_id=1, source_target_pairs={{4,0},{8,4},{12,8},{16,12},{20,16},{24,20},{28,24},{0,28},{5,1},{9... | collective-permute-start | bytes 27656 | tf_op jit(solution)/shard_map/ppermute | solution.py:34
  41.8 9.0 %collective-permute-start.4 = (f32[12,12,2,12]{3,2,1,0:T(2,128)S(1)}, f32[12,12,2,12]{3,2,1,0:T(2,128)S(1)}, u32[]{:S(2)}, u32[]{:S(2)}) collective-permute-start(f32[12,12,2,12]{3,2,1,0:T(2,128)S(1)} %get-tuple-element.61), channel_id=1, source_target_pairs={{0,1},{1,2},{2,3},{3,0},{4,5},{5,6},{6,7},{7,4},{8,9},{9,10},{10,1... | collective-permute-start | bytes 41480 | tf_op jit(solution)/shard_map/ppermute | solution.py:33
  43.8 7.1 %collective-permute-start.5 = (f32[12,12,2,12]{3,2,1,0:T(2,128)S(1)}, f32[12,12,2,12]{3,2,1,0:T(2,128)S(1)}, u32[]{:S(2)}, u32[]{:S(2)}) collective-permute-start(f32[12,12,2,12]{3,2,1,0:T(2,128)S(1)} %get-tuple-element.62), channel_id=1, source_target_pairs={{1,0},{2,1},{3,2},{0,3},{5,4},{6,5},{7,6},{4,7},{9,8},{10,9},{11,1... | collective-permute-start | bytes 41480 | tf_op jit(solution)/shard_map/ppermute | solution.py:34
  51.2 1.4 %copy-start.1 = (f32[12,12,12,12]{3,2,1,0:T(8,128)}, f32[12,12,12,12]{3,2,1,0:T(8,128)S(1)}, u32[]{:S(2)}) copy-start(f32[12,12,12,12]{3,2,1,0:T(8,128)S(1)} %pad_maximum_fusion) | copy-start | bytes 248836
  57.3 3.7 %copy-start.3 = (f32[12,64]{1,0:T(8,128)S(1)}, f32[12,64]{1,0:T(8,128)}, u32[]{:S(2)}) copy-start(f32[12,64]{1,0:T(8,128)} %param.20) | copy-start | bytes 9220
  57.3 4.0 %copy-start.5 = (f32[64,64]{1,0:T(8,128)S(1)}, f32[64,64]{1,0:T(8,128)}, u32[]{:S(2)}) copy-start(f32[64,64]{1,0:T(8,128)} %param.21) | copy-start | bytes 49156
  57.4 4.3 %copy-start.2 = (f32[64,64]{1,0:T(8,128)S(1)}, f32[64,64]{1,0:T(8,128)}, u32[]{:S(2)}) copy-start(f32[64,64]{1,0:T(8,128)} %param.22) | copy-start | bytes 49156
  64.0 2.0 %copy-start.6 = (f32[64]{0:T(128)S(1)}, f32[64]{0:T(128)}, u32[]{:S(2)}) copy-start(f32[64]{0:T(128)} %param.24) | copy-start | bytes 772
  86.4 12.7 %collective-permute-start.6 = (f32[2,12,12,9]{2,0,3,1:T(2,128)S(1)}, f32[2,12,12,9]{2,0,3,1:T(2,128)S(1)}, u32[]{:S(2)}, u32[]{:S(2)}) collective-permute-start(f32[2,12,12,9]{2,0,3,1:T(2,128)S(1)} %bitcast.107), channel_id=1, source_target_pairs={{0,32},{32,64},{64,96},{96,128},{128,160},{160,192},{192,224},{224... | collective-permute-start | bytes 31112 | tf_op jit(solution)/shard_map/ppermute | solution.py:23
  93.5 12.2 %collective-permute-start.7 = (f32[2,12,12,9]{2,0,3,1:T(2,128)S(1)}, f32[2,12,12,9]{2,0,3,1:T(2,128)S(1)}, u32[]{:S(2)}, u32[]{:S(2)}) collective-permute-start(f32[2,12,12,9]{2,0,3,1:T(2,128)S(1)} %bitcast.108), channel_id=1, source_target_pairs={{0,992},{32,0},{64,32},{96,64},{128,96},{160,128},{192,160},{224,1... | collective-permute-start | bytes 31112 | tf_op jit(solution)/shard_map/ppermute | solution.py:23
  105.8 7.8 %collective-permute-start.8 = (f32[8,2,12,9]{2,0,3,1:T(8,128)S(1)}, f32[8,2,12,9]{2,0,3,1:T(8,128)S(1)}, u32[]{:S(2)}, u32[]{:S(2)}) collective-permute-start(f32[8,2,12,9]{2,0,3,1:T(8,128)S(1)} %get-tuple-element.70), channel_id=1, source_target_pairs={{0,4},{4,8},{8,12},{12,16},{16,20},{20,24},{24,28},{28,0},{1,5},{5... | collective-permute-start | bytes 20744 | tf_op jit(solution)/shard_map/ppermute | solution.py:23
  107.7 7.5 %collective-permute-start.9 = (f32[8,2,12,9]{2,0,3,1:T(8,128)S(1)}, f32[8,2,12,9]{2,0,3,1:T(8,128)S(1)}, u32[]{:S(2)}, u32[]{:S(2)}) collective-permute-start(f32[8,2,12,9]{2,0,3,1:T(8,128)S(1)} %get-tuple-element.71), channel_id=1, source_target_pairs={{0,28},{4,0},{8,4},{12,8},{16,12},{20,16},{24,20},{28,24},{1,29},{... | collective-permute-start | bytes 20744 | tf_op jit(solution)/shard_map/ppermute | solution.py:23
  115.4 8.3 %collective-permute-start.10 = (f32[8,8,2,9]{2,0,3,1:T(8,128)S(1)}, f32[8,8,2,9]{2,0,3,1:T(8,128)S(1)}, u32[]{:S(2)}, u32[]{:S(2)}) collective-permute-start(f32[8,8,2,9]{2,0,3,1:T(8,128)S(1)} %get-tuple-element.72), channel_id=1, source_target_pairs={{0,1},{1,2},{2,3},{3,0},{4,5},{5,6},{6,7},{7,4},{8,9},{9,10},{10,1... | collective-permute-start | bytes 13832 | tf_op jit(solution)/shard_map/ppermute | solution.py:23
  117.3 7.9 %collective-permute-start.11 = (f32[8,8,2,9]{2,0,3,1:T(8,128)S(1)}, f32[8,8,2,9]{2,0,3,1:T(8,128)S(1)}, u32[]{:S(2)}, u32[]{:S(2)}) collective-permute-start(f32[8,8,2,9]{2,0,3,1:T(8,128)S(1)} %get-tuple-element.73), channel_id=1, source_target_pairs={{0,3},{1,0},{2,1},{3,2},{4,7},{5,4},{6,5},{7,6},{8,11},{9,8},{10,9... | collective-permute-start | bytes 13832 | tf_op jit(solution)/shard_map/ppermute | solution.py:23
where the time goes:
time: 129 us; the launch traced here: 127 us
  starting transfers between devices  54.7 us (42%)
  local copies, waits for them, and re-layouts  28.1 us (22%)
  other arithmetic  22.3 us (17%)
  waiting for transfers between devices  16.1 us (12%)
  matrix products  3.46 us (3%)
  between operations  2.03 us (2%)
    ppermute x6, starting transfers between devices, shifted(): lax.ppermute(shard, axis, [(i, (i + by) % length) for i in range(length)])  21.4 us
    ppermute x3, starting transfers between devices, with_halo(): after = lax.ppermute(first, axis, down)  20.4 us
    ppermute x3, starting transfers between devices, with_halo(): before = lax.ppermute(last, axis, up)  12.8 us
    ppermute x6, waiting for transfers between devices, shifted(): lax.ppermute(shard, axis, [(i, (i + by) % length) for i in range(length)])  12 us
    scatter-add x1, other arithmetic, one_block(): forces = forces.at[:, first].add(grad)  5.01 us
    slice x2, local copies, waits for them, and re-layouts, fold_layers(): inner = lax.slice_in_dim(values, 2, length - 2, axis=axis_dim)  3.7 us
    ppermute x3, waiting for transfers between devices, with_halo(): after = lax.ppermute(first, axis, down)  3.44 us
    add x1, local copies, waits for them, and re-layouts, local(): corner[:, :, :, None, :] + sites[None, None, None, :, :] + shifts  3.33 us
  transfers between devices with their start and end apart: 12, of which 8 were waited for; matrix products, arithmetic and copies ran while one was open for 12% of the time, Pallas kernels for 0%

commit v1 on v0

v1 whole, which is shorter than its diff:
```python
import math

import jax
import jax.numpy as jnp
import numpy as np
from jax import lax
from jax.experimental import pallas as pl
from jax.experimental.pallas import tpu as pltpu
from jax.sharding import PartitionSpec as P

F32 = jnp.float32
BF16 = jnp.bfloat16
CELL = 3.1
CUT = 6.0
VM = pl.BlockSpec(memory_space=pltpu.VMEM)
SM = pl.BlockSpec(memory_space=pltpu.SMEM)
LANES = 144
PAIRS = 512
NS = 16


def call(kernel, outs, ins, name, scratch=(), flops=0):
    specs = [s for _, s in ins]
    return pl.pallas_call(
        kernel,
        out_shape=outs,
        in_specs=specs,
        out_specs=jax.tree.map(lambda _: VM, outs),
        scratch_shapes=list(scratch),
        name=name,
        cost_estimate=pl.CostEstimate(flops=flops, bytes_accessed=0, transcendentals=0),
    )(*[a for a, _ in ins])


def split(v, parts):
    out = []
    for _ in range(parts - 1):
        h = v.astype(BF16)
        out.append(h)
        v = v - h.astype(F32)
    out.append(v.astype(BF16))
    return out


def mm(a, b, dims=((1,), (0,))):
    return lax.dot_general(a, b, (dims, ((), ())), preferred_element_type=F32)


def pack_kernel(d_ref, s_ref, o_ref):
    for i in range(36):
        o_ref[i : i + 1, :] = d_ref[0, :, 128 * i : 128 * i + 128]
    for i in range(12):
        o_ref[36 + i : 37 + i, :] = s_ref[0, :, 128 * i : 128 * i + 128].astype(F32)


def zperm():
    m = np.zeros((3, 128, 256), np.float32)
    for s in range(12):
        d, z = (1, s + 6) if s < 2 else ((0, s - 2) if s < 10 else (2, s - 10))
        for a in range(3):
            for c in range(3):
                m[d, z * 9 + a * 3 + c, s * 12 + a * 4 + c] = 1.0
            m[d, 72 + z * 3 + a, s * 12 + a * 4 + 3] = 1.0
    return m.reshape(384, 256)


def zrows_kernel(e_ref, g_ref, p_ref, o_ref, lo_ref, hi_ref, t_ref):
    e = e_ref[0]
    lane = lax.broadcasted_iota(jnp.int32, (4, 128), 1)
    for d in range(3):
        at = lax.rem(e + (0, 3, 1)[d], 4)
        for j in range(16):
            r, off = divmod(72 * j, 128)
            v = g_ref[at, pl.ds(r, 4, stride=9), :]
            v = pltpu.roll(v, (128 - off) % 128, axis=1) if off else v
            if off + 72 > 128:
                n = g_ref[at, pl.ds(r + 1, 4, stride=9), :]
                n = pltpu.roll(n, 128 - off, axis=1)
                v = jnp.where(lane < 128 - off, v, n)
            r, off = divmod(24 * j, 128)
            k = g_ref[at, pl.ds(36 + r, 4, stride=3), :]
            k = pltpu.roll(k, (72 - off) % 128, axis=1)
            if off + 24 > 128:
                n = g_ref[at, pl.ds(37 + r, 4, stride=3), :]
                n = pltpu.roll(n, (72 - off) % 128, axis=1)
                k = jnp.where(lane < 72 + 128 - off, k, n)
            v = jnp.where(lane < 72, v, jnp.where(lane < 96, k, 0.0))
            t_ref[d, pl.ds(j, 4, stride=16), :] = v
    rows = jnp.concatenate([t_ref[0], t_ref[1], t_ref[2]], axis=1)
    r = mm(jnp.concatenate(split(rows, 3), axis=0), p_ref[...])
    r = (r[0:64] + r[64:128]) + r[128:192]
    for h in range(2):
        v = r[:, 128 * h : 128 * h + 128]
        o_ref[h] = v
        lo_ref[h] = v[0:16]
        hi_ref[h] = v[48:64]


def yslab_kernel(o_ref, m_ref, p_ref, lo_ref, hi_ref):
    for out, base in ((lo_ref, 0), (hi_ref, 6)):
        for h in range(2):
            for k in range(2):
                out[h, 8 * k : 8 * k + 8, :] = o_ref[h, pl.ds(base + k, 8, stride=8), :]
                out[h, 16 + 4 * k : 18 + 4 * k, :] = m_ref[h, pl.ds(base + k, 2, stride=8), :]
                out[h, 18 + 4 * k : 20 + 4 * k, :] = p_ref[h, pl.ds(base + k, 2, stride=8), :]


def weights_kernel(w2, wl, we, wo, ro, t2, tl, te, to, bo, be, bl, b2, rc):
    def three(w):
        h, l = split(w, 2)
        return jnp.concatenate([h, h, l], axis=1)

    pad = jnp.concatenate([w2[...], jnp.zeros((4, 64), F32)], axis=0)
    t2[...] = three(pad.T)
    tl[...] = three(wl[...].T)
    te[...] = three(we[...].T)
    to[...] = three(wo[...].T)
    bo[...] = three(wo[...])
    be[...] = three(we[...])
    bl[...] = three(wl[...])
    b2[...] = three(w2[4:12, :])
    eye = lax.broadcasted_iota(jnp.int32, (64, 64), 0) == lax.broadcasted_iota(
        jnp.int32, (64, 64), 1
    )
    rc[...] = jnp.sum(jnp.where(eye, jnp.broadcast_to(ro[...], (64, 64)), 0.0), axis=1, keepdims=True)


def index_kernel(alive_ref, nb_ref, ce_ref, ct_ref, oh_ref, geo_ref):
    nb = nb_ref[...].astype(F32)
    ce = ce_ref[...].astype(F32)

    def div(v, k):
        return jnp.floor((v + 0.5) * (1.0 / k))

    pq = div(nb, 36)
    r = nb - 36.0 * pq
    p = div(pq, 12)
    q = pq - 12.0 * p
    s = div(r, 3)
    a = r - 3.0 * s
    inx = (p >= 2.0) & (p < 10.0)
    px = jnp.where(p < 2.0, p, p - 8.0)
    row_in = jnp.where(inx, (p - 2.0) * 8.0, jnp.where(p < 2.0, 64.0 + 8.0 * p, 80.0 + 8.0 * (p - 10.0)))
    row_in = row_in + (q - 2.0)
    qy = jnp.where(q < 2.0, q, q - 10.0)
    row_y = jnp.where(inx, 8.0 * qy + (p - 2.0), 16.0 + 4.0 * qy + px)
    row = jnp.where(q < 2.0, 96.0 + row_y, jnp.where(q < 10.0, row_in, 120.0 + row_y))

    cell = div(ce, 3)
    ca = ce - 3.0 * cell
    cxy = div(cell, 8)
    cz = cell - 8.0 * cxy
    cx = div(cxy, 8)
    cy = cxy - 8.0 * cx
    cr = (cz + 2.0) * 3.0 + ca

    def place(x, y, z, atom):
        return (
            x + jnp.where(atom == 1.0, 0.75, 0.25),
            y + jnp.where(atom >= 1.0, 0.75, 0.25),
            z + jnp.where(atom == 2.0, 0.75, 0.25),
        )

    second = place(p - 2.0, q - 2.0, s - 2.0, a)
    first = place(cx, cy, cz, ca)
    for k in range(3):
        geo_ref[k : k + 1, 0:PAIRS] = second[k] - jnp.concatenate([first[k]] * 4, axis=1)
    lane = lax.broadcasted_iota(jnp.int32, (1, PAIRS), 1)
    slot = lax.shift_right_logical(lane, 4)
    centre = lane & 15
    count = jnp.concatenate([ct_ref[...]] * 4, axis=1)
    live = (slot < count) & (centre < alive_ref[0])
    geo_ref[3:4, 0:PAIRS] = jnp.where(live, 1.0, 0.0)
    rows = jnp.concatenate([row, cxy], axis=1)
    geo_ref[4:5, :] = jnp.concatenate([r, cr], axis=1)
    at = lax.broadcasted_iota(jnp.int32, (LANES, PAIRS + 128), 0).astype(F32)
    oh_ref[...] = jnp.where(at == rows, 1.0, 0.0).astype(BF16)


def poly(x, coefs):
    acc = jnp.full_like(x, coefs[-1])
    for c in coefs[-2::-1]:
        acc = acc * x + c
    return acc


SIN = [math.pi ** (2 * k + 1) * (-1) ** k / math.factorial(2 * k + 1) for k in range(7)]
COS = [math.pi ** (2 * k) * (-1) ** k / math.factorial(2 * k) for k in range(8)]
R3, R5, R15 = math.sqrt(3.0), math.sqrt(5.0), math.sqrt(15.0)
ORDER = (0, 1, 1, 1, 2, 2, 2, 2, 2)


def stack3(v):
    h, l = split(v, 2)
    return jnp.concatenate([h, l, h], axis=0)


def slots_sum(v):
    t = (v[:, 0:128] + v[:, 128:256]) + (v[:, 256:384] + v[:, 384:512])
    for by in (16, 32, 64):
        t = t + pltpu.roll(t, by, axis=1)
    return t


def four(v):
    return jnp.concatenate([v] * 4, axis=1)


def main_kernel(
    oh_ref, geo_ref, o_ref, xm_ref, xp_ref, ym_ref, yp_ref,
    t2, tl, te, to, bo, be, bl, b2, rc,
    en_ref, fo_ref, fxm_ref, fxp_ref, fym_ref, fyp_ref,
    w_s, q_s, g_s, a_s, in_s, dw_s, sc_s,
):
    refs = (o_ref, xm_ref, xp_ref, ym_ref, yp_ref)
    tt = jnp.concatenate(
        [
            jnp.concatenate([v[0] for v in refs], axis=0).T,
            jnp.concatenate([v[1] for v in refs], axis=0).T[0 : LANES - 128],
        ],
        axis=0,
    )
    hot = oh_ref[...]
    got = mm(jnp.concatenate(split(tt, 2), axis=0), hot)
    rsel = geo_ref[4:5, :]
    sub = lax.broadcasted_iota(jnp.int32, (8, PAIRS + 128), 0)
    half = lax.shift_right_logical(sub, 2).astype(F32)
    pick = jnp.zeros((8, PAIRS + 128), F32)
    for k in range(18):
        v = got[8 * k : 8 * k + 8] + got[LANES + 8 * k : LANES + 8 * k + 8]
        pick = jnp.where(half + 2.0 * k == rsel, v, pick)
    pick = pick[0:4] + pick[4:8]
    first = four(pick[:, PAIRS:])
    second = pick[:, 0:PAIRS]
    geo = geo_ref[...]
    live = geo[3:4, 0:PAIRS]
    rx = [(geo[k : k + 1, 0:PAIRS] + (second[k : k + 1] - first[k : k + 1])) * CELL for k in range(3)]
    d2 = rx[0] * rx[0] + rx[1] * rx[1] + rx[2] * rx[2]
    inv = lax.rsqrt(d2)
    inv = inv * (1.5 - 0.5 * d2 * inv * inv)
    dist = d2 * inv
    ux, uy, uz = [v * inv for v in rx]
    x = dist * (1.0 / CUT)
    inside = x < 1.0
    x = jnp.minimum(x, 1.0)
    x2 = x * x
    x3 = x2 * x
    x5 = x3 * x2
    x6 = x3 * x3
    env = jnp.where(inside, 1.0 + x6 * (-28.0 + x * (48.0 - 21.0 * x)), 0.0)
    denv_dd = jnp.where(inside, (-168.0 / CUT) * x5 * (1.0 - x) * (1.0 - x), 0.0)
    ev = env * live

    n = (lax.broadcasted_iota(jnp.int32, (8, PAIRS), 0) + 1).astype(F32)
    t = n * x
    k = jnp.floor(t + 0.5)
    f = t - k
    sign = 1.0 - 2.0 * (k - 2.0 * jnp.floor(k * 0.5))
    f2 = f * f
    sn = sign * f * poly(f2, SIN)
    cs = sign * poly(f2, COS)
    c0 = math.sqrt(2.0 / CUT)
    sd = sn * (c0 * inv)
    basis = sd * env
    dbasis = (n * cs) * ((c0 * math.pi / CUT) * inv * env) + sd * (denv_dd - env * inv)
    k1, k2 = first[3:4], second[3:4]
    in_s[0:1, :] = jnp.where(k1 == 0.0, 1.0, 0.0)
    in_s[1:2, :] = jnp.where(k1 == 1.0, 1.0, 0.0)
    in_s[2:3, :] = jnp.where(k2 == 0.0, 1.0, 0.0)
    in_s[3:4, :] = jnp.where(k2 == 1.0, 1.0, 0.0)
    in_s[4:12, :] = basis
    in_s[12:16, :] = jnp.zeros((4, PAIRS), F32)

    def silu(v):
        sg = 1.0 / (1.0 + jnp.exp(-v))
        return v * sg, sg * (1.0 + v * (1.0 - sg))

    h, dh_ = silu(mm(t2[...], stack3(in_s[...])))
    z, dz_ = silu(mm(tl[...], stack3(h)))
    zs = stack3(z)
    e = mm(te[...], zs)
    w_s[...] = e * ev

    ys = [
        None, R3 * ux, R3 * uy, R3 * uz, R15 * ux * uy, R15 * uy * uz,
        (0.5 * R5) * (3.0 * uz * uz - 1.0), R15 * ux * uz, (0.5 * R15) * (ux * ux - uy * uy),
    ]
    yb = [None] + [jnp.broadcast_to(v, (8, PAIRS)) for v in ys[1:]]
    for c in range(8):
        at = slice(8 * c, 8 * c + 8)
        w = w_s[at, :]
        sums = [None, None, None]
        for m in range(9):
            am = 0.2 * slots_sum(w if m == 0 else w * yb[m])
            a_s[m, at, :] = am
            am = four(am)
            term = am if m == 0 else yb[m] * am
            l = ORDER[m]
            sums[l] = term if sums[l] is None else sums[l] + term
        for l in range(3):
            q_s[l, at, :] = sums[l]
    wv = w_s[...]
    joined = jnp.concatenate([z] + [wv * q_s[l] for l in range(3)], axis=0)
    y, dy_ = silu(mm(to[...], stack3(joined)))
    ro = rc[...]
    raw = jnp.sum(ro * y, axis=0, keepdims=True)
    en = slots_sum(raw * ev)
    en_ref[...] = en[:, 0:NS].reshape(1, 1, NS)
    denv = live * raw
    dj = mm(bo[...], stack3((ro * ev) * dy_))
    g_s[...] = dj[64:256]
    acc = [None] * 9
    for c in range(8):
        at = slice(8 * c, 8 * c + 8)
        w = w_s[at, :]
        dw = None
        for l in range(3):
            g = g_s[64 * l + 8 * c : 64 * l + 8 * c + 8, :]
            part = g * q_s[l, at, :]
            dw = part if dw is None else dw + part
            gw = g * w
            for m in range(9):
                if ORDER[m] != l:
                    continue
                bm = four(0.2 * slots_sum(gw if m == 0 else gw * yb[m]))
                dw = dw + (bm if m == 0 else yb[m] * bm)
                if m:
                    v = gw * four(a_s[m, at, :]) + w * bm
                    acc[m] = v if acc[m] is None else acc[m] + v
        dw_s[at, :] = dw
    dw = dw_s[...]
    denv = denv + live * jnp.sum(dw * e, axis=0, keepdims=True)
    dz = dj[0:64] + mm(be[...], stack3(dw * ev))
    dh = mm(bl[...], stack3(dz * dz_))
    db = mm(b2[...], stack3(dh * dh_))
    dd = denv * denv_dd + jnp.sum(db * dbasis, axis=0, keepdims=True)
    dy = [None] + [jnp.sum(acc[m], axis=0, keepdims=True) for m in range(1, 9)]
    du0 = R3 * dy[1] + R15 * (uy * dy[4] + uz * dy[7] + ux * dy[8])
    du1 = R3 * dy[2] + R15 * (ux * dy[4] + uz * dy[5] - uy * dy[8])
    du2 = R3 * dy[3] + R15 * (uy * dy[5] + ux * dy[7]) + (3.0 * R5) * uz * dy[6]
    along = ux * du0 + uy * du1 + uz * du2
    dd = dd - along * inv
    grad = [du0 * inv + ux * dd, du1 * inv + uy * dd, du2 * inv + uz * dd]

    lane = lax.broadcasted_iota(jnp.int32, (1, 128), 1)
    sc_s[...] = jnp.zeros((8, PAIRS + 128), F32)
    for k in range(3):
        own = jnp.where(lane < NS, slots_sum(grad[k]), 0.0)
        for row in (k, k + 4):
            sc_s[row : row + 1, 0:PAIRS] = -grad[k]
            sc_s[row : row + 1, PAIRS:] = own
    gv = sc_s[...]
    m = jnp.concatenate(
        [jnp.where(half + 2.0 * k == rsel, gv, 0.0) for k in range(18)]
        + [jnp.zeros((256 - LANES, PAIRS + 128), F32)],
        axis=0,
    )
    mh, ml = split(m, 2)
    nt = ((1,), (1,))
    out = mm(hot, mh, nt) + mm(hot, ml, nt)
    for h in range(2):
        v = out[:, 128 * h : 128 * h + 128]
        fo_ref[h] = v[0:64]
        fxm_ref[h] = v[64:80]
        fxp_ref[h] = v[80:96]
        fym_ref[h] = v[96:120]
        fyp_ref[h] = v[120:144]


def yfold_kernel(fo, fm, fp, lo, hi, o_ref, m_ref, p_ref):
    o_ref[...] = fo[...]
    m_ref[...] = fm[...]
    p_ref[...] = fp[...]
    for got, base in ((lo, 0), (hi, 6)):
        for k in range(2):
            for ref, a, n in ((o_ref, 8 * k, 8), (m_ref, 16 + 4 * k, 2), (p_ref, 18 + 4 * k, 2)):
                at = pl.ds(base + k, n, stride=8)
                for h in range(2):
                    ref[h, at, :] = ref[h, at, :] + got[h, a : a + n, :]


def xfold_kernel(fo, lo, hi, o_ref, z_ref):
    a, b = [
        jnp.concatenate([fo[h, 0:16, :] + lo[h], fo[h, 16:48, :], fo[h, 48:64, :] + hi[h]], axis=0)
        for h in range(2)
    ]
    o_ref[...] = a
    lane = lax.broadcasted_iota(jnp.int32, (64, 128), 1)
    b = pltpu.roll(b, 24, axis=1)
    z_ref[...] = jnp.where(
        lane < 24, a, jnp.where(lane < 40, b, jnp.where(lane < 120, 0.0, a))
    )


def fperm():
    m = np.zeros((128, 128), np.float32)
    for z in range(8):
        for a in range(3):
            for c in range(3):
                m[24 + z * 12 + a * 4 + c, z * 9 + a * 3 + c] = 1.0
    return m


def zfold_kernel(e_ref, f_ref, g_ref, p_ref, o_ref, t_ref):
    e = e_ref[0]
    lane = lax.broadcasted_iota(jnp.int32, (64, 128), 1)
    above = g_ref[lax.rem(e + 1, 4)]
    below = g_ref[lax.rem(e + 3, 4)]
    f = f_ref[...]
    f = f + jnp.where((lane >= 96) & (lane < 120), pltpu.roll(above, 96, axis=1), 0.0)
    low = jnp.where(lane < 32, pltpu.roll(below, 32, axis=1), pltpu.roll(below, 8, axis=1))
    f = f + jnp.where((lane >= 24) & (lane < 48), low, 0.0)
    r = mm(jnp.concatenate(split(f, 3), axis=0), p_ref[...])
    t_ref[...] = (r[0:64] + r[64:128]) + r[128:192]
    lane = lax.broadcasted_iota(jnp.int32, (4, 128), 1)
    for k in range(9):
        v = jnp.zeros((4, 128), F32)
        for j in range(128 * k // 72, (128 * k + 127) // 72 + 1):
            off = 72 * j - 128 * k
            part = pltpu.roll(t_ref[pl.ds(j, 4, stride=16), :], off % 128, axis=1)
            v = v + jnp.where((lane >= off) & (lane < off + 72), part, 0.0)
        for g in range(4):
            o_ref[0, :, 128 * (9 * g + k) : 128 * (9 * g + k) + 128] = v[g : g + 1]


def sds(shape, dtype=F32):
    return jax.ShapeDtypeStruct(shape, dtype)


def hop(v, axis, by):
    n = lax.axis_size(axis)
    return lax.ppermute(v, axis, [(i, (i + by) % n) for i in range(n)])


def local(
    displacement, species, centres, neighbours, neighbour_count, live_centres,
    w_two, w_lat, w_env, w_out, readout,
):
    e = lax.axis_index("gz").astype(jnp.int32).reshape(1)
    flat = call(pack_kernel, sds((48, 128)), [(displacement, VM), (species, VM)], "pack")
    column = lax.all_gather(flat, "gz")
    slab = sds((2, 16, 128))
    own, lo, hi = call(
        zrows_kernel,
        (sds((2, 64, 128)), slab, slab),
        [(e, SM), (column, VM), (jnp.asarray(zperm(), BF16), VM)],
        "zrows",
        [pltpu.VMEM((3, 64, 128), F32)],
    )
    xm, xp = hop(hi, "gx", 1), hop(lo, "gx", -1)

    ws = call(
        weights_kernel,
        (
            sds((64, 48), BF16), sds((64, 192), BF16), sds((64, 192), BF16), sds((64, 768), BF16),
            sds((256, 192), BF16), sds((64, 192), BF16), sds((64, 192), BF16), sds((8, 192), BF16),
            sds((64, 1)),
        ),
        [(w_two, VM), (w_lat, VM), (w_env, VM), (w_out, VM), (readout.reshape(1, 64), VM)],
        "weights",
    )
    hot, geo = call(
        index_kernel,
        (sds((LANES, PAIRS + 128), BF16), sds((8, PAIRS + 128))),
        [
            (live_centres.reshape(1), SM),
            (neighbours.reshape(NS, 32).T.reshape(1, PAIRS), VM),
            (jnp.tile(centres.reshape(1, NS), (1, 8)), VM),
            (jnp.tile(neighbour_count.reshape(1, NS), (1, 8)), VM),
        ],
        "index",
    )

    slab = sds((2, 24, 128))
    lo, hi = call(yslab_kernel, (slab, slab), [(own, VM), (xm, VM), (xp, VM)], "yslab")
    ym, yp = hop(hi, "gy", 1), hop(lo, "gy", -1)

    en, fo, fxm, fxp, fym, fyp = call(
        main_kernel,
        (
            sds((1, 1, NS)), sds((2, 64, 128)), sds((2, 16, 128)), sds((2, 16, 128)),
            sds((2, 24, 128)), sds((2, 24, 128)),
        ),
        [(v, VM) for v in (hot, geo, own, xm, xp, ym, yp, *ws)],
        "pairs",
        [
            pltpu.VMEM((64, PAIRS), F32), pltpu.VMEM((3, 64, PAIRS), F32),
            pltpu.VMEM((192, PAIRS), F32), pltpu.VMEM((9, 64, 128), F32),
            pltpu.VMEM((16, PAIRS), F32), pltpu.VMEM((64, PAIRS), F32),
            pltpu.VMEM((8, PAIRS + 128), F32),
        ],
    )
    hi, lo = hop(fym, "gy", -1), hop(fyp, "gy", 1)
    fo, fxm, fxp = call(
        yfold_kernel,
        (sds((2, 64, 128)), sds((2, 16, 128)), sds((2, 16, 128))),
        [(v, VM) for v in (fo, fxm, fxp, lo, hi)],
        "yfold",
    )
    hi, lo = hop(fxm, "gx", -1), hop(fxp, "gx", 1)
    fo, z = call(
        xfold_kernel, (sds((64, 128)), sds((64, 128))), [(fo, VM), (lo, VM), (hi, VM)], "xfold"
    )
    column = lax.all_gather(z, "gz")
    out = call(
        zfold_kernel,
        sds((1, 1, 4608)),
        [(e, SM), (fo, VM), (column, VM), (jnp.asarray(fperm(), BF16), VM)],
        "zfold",
        [pltpu.VMEM((64, 128), F32)],
    )
    return en, out


def solution(mesh):
    cut = P("gx", "gy", "gz")
    return jax.shard_map(
        local,
        mesh=mesh,
        in_specs=(cut,) * 6 + (P(),) * 5,
        out_specs=(cut, cut),
        check_vma=False,
    )
```

time: 129 us -> 96.1 us (0.74)
  local copies, waits for them, and re-layouts: 28.1 us -> 5.83 us
  other arithmetic: 22.3 us -> 0.71 us
  Pallas kernels: 0 us -> 18.3 us
  starting transfers between devices: 54.7 us -> 39 us
  blocking collectives: 0 us -> 13.6 us
  matrix products: 3.46 us -> 0 us
    pallas_call x0 -> x9, Pallas kernels: none -> 18.3 us  [call(): pl.pallas_call(kernel, out_shape=outs, in_specs=specs, out_specs=jax.tree...]
    ppermute x12 -> x8, starting transfers between devices: 54.7 us -> 39 us  [hop(): return lax.ppermute(v, axis, [(i, (i + by) % n) for i in range(n)])]
    all_gather x0 -> x2, blocking collectives: none -> 13.6 us  [the longest x1 6.97 us: local(): column = lax.all_gather(flat, 'gz')]
    reshape x10 -> x3, local copies, waits for them, and re-layouts: 9.53 us -> 0.82 us  [local(): neighbours.reshape(NS, 32).T.reshape(1, PAIRS)]
    scatter-add x2 -> x0, other arithmetic: 8.13 us -> none  [the longest x1 5.01 us: one_block(): forces = forces.at[:, first].add(grad)]
    slice x11 -> x0, local copies, waits for them, and re-layouts: 7.79 us -> none  [the longest x2 3.7 us: fold_layers(): inner = lax.slice_in_dim(values, 2, length - 2, axis=axis_dim)]
    reduce_sum x10 -> x0, other arithmetic: 4.43 us -> none  [the longest x1 1.56 us: block_energy(): harm[:, None, :] * weights[None, :, :]]
    add x5 -> x0, other arithmetic: 4.03 us -> none  [the longest x1 2.97 us: local(): corner[:, :, :, None, :] + sites[None, None, None, :, :] + shifts]
  transfers between devices with their start and end apart: 12 -> 8, of which waited for: 8 -> 4; matrix products, arithmetic and copies ran while one was open for 12% -> 4% of each run, Pallas kernels for 0% -> 3%
where the time goes in v1:
time: 96.1 us; the launch traced here: 94.7 us
  starting transfers between devices  39 us (41%)
  Pallas kernels  18.3 us (19%)
  waiting for transfers between devices  15.9 us (17%)
  blocking collectives  13.6 us (14%)
  local copies, waits for them, and re-layouts  5.83 us (6%)
  between operations  1.43 us (1%)
    ppermute x8, starting transfers between devices, hop(): return lax.ppermute(v, axis, [(i, (i + by) % n) for i in range(n)])  39 us
    pallas_call x9, Pallas kernels, call(): pl.pallas_call(kernel, out_shape=outs, in_specs=specs, out_specs=jax.tree...  18.3 us
    ppermute x8, waiting for transfers between devices, hop(): return lax.ppermute(v, axis, [(i, (i + by) % n) for i in range(n)])  15.9 us
    all_gather x1, blocking collectives, local(): column = lax.all_gather(flat, 'gz')  6.97 us
    all_gather x1, blocking collectives, local(): column = lax.all_gather(z, 'gz')  6.64 us
    unnamed x26, local copies, waits for them, and re-layouts  3.77 us
  transfers between devices with their start and end apart: 8, of which 4 were waited for; matrix products, arithmetic and copies ran while one was open for 4% of the time, Pallas kernels for 3%

profile of v1, /device:TPU:46, one launch (start us, length us, event | category | flops | bytes accessed | tf_op | source)
XLA Modules:
  0.0 94.7 jit_solution(7179307139666481929)
XLA Ops:
  0.6 1.3 %pack.1 = f32[48,128]{1,0:T(8,128)} custom-call(f32[1,1,4608]{2,1,0:T(1,128)} %d_ref.1, s32[1,1,1536]{2,1,0:T(1,128)} %s_ref.1), custom_call_target="tpu_custom_call" | custom-call | tf_op jit(solution)/shard_map/pack/pallas_call | solution.py:24
  2.0 7.0 %all-gather = f32[192,128]{1,0:T(8,128)} all-gather(f32[48,128]{1,0:T(8,128)} %pack.1), channel_id=2, replica_groups=mesh['gx'=32,'gy'=8,'gz'=4] {'gz'}, dimensions={0}, use_global_device_ids=true | all-gather | bytes 122880 | tf_op jit(solution)/shard_map/all_gather | solution.py:441
  8.9 2.0 %zrows.1 = (f32[2,64,128]{2,1,0:T(8,128)}, f32[2,16,128]{2,1,0:T(8,128)}, f32[2,16,128]{2,1,0:T(8,128)}) custom-call(s32[1]{0:T(128)} %bitcast.4.e_ref, f32[4,48,128]{2,1,0:T(8,128)} %bitcast.10, bf16[384,256]{1,0:T(8,128)(2,1)} %constant.8.clone.p_ref), custom_call_target="tpu_custom_call" | custom-call | tf_op jit(solution)/shard_map/zrows/pallas_call | solution.py:24
  10.9 4.8 %collective-permute-start = (f32[2,16,128]{2,1,0:T(8,128)}, f32[2,16,128]{2,1,0:T(8,128)S(1)}, u32[]{:S(2)}, u32[]{:S(2)}) collective-permute-start(f32[2,16,128]{2,1,0:T(8,128)} %get-tuple-element.32), channel_id=1, source_target_pairs={{0,32},{32,64},{64,96},{96,128},{128,160},{160,192},{192,224},{224... | collective-permute-start | bytes 49160 | tf_op jit(solution)/shard_map/ppermute | solution.py:432
  15.8 1.9 %collective-permute-start.1 = (f32[2,16,128]{2,1,0:T(8,128)}, f32[2,16,128]{2,1,0:T(8,128)S(1)}, u32[]{:S(2)}, u32[]{:S(2)}) collective-permute-start(f32[2,16,128]{2,1,0:T(8,128)} %get-tuple-element.33), channel_id=1, source_target_pairs={{0,992},{32,0},{64,32},{96,64},{128,96},{160,128},{192,160},{224,1... | collective-permute-start | bytes 49160 | tf_op jit(solution)/shard_map/ppermute | solution.py:432
  17.7 8.1 %collective-permute-done.1.p_ref.xp_ref = f32[2,16,128]{2,1,0:T(8,128)S(1)} collective-permute-done((f32[2,16,128]{2,1,0:T(8,128)}, f32[2,16,128]{2,1,0:T(8,128)S(1)}, u32[]{:S(2)}, u32[]{:S(2)}) %collective-permute-start.1) | collective-permute-done | bytes 16416 | tf_op jit(solution)/shard_map/ppermute | solution.py:432
  25.8 0.6 copy-done.2
  26.4 1.5 %yslab.1 = (f32[2,24,128]{2,1,0:T(8,128)}, f32[2,24,128]{2,1,0:T(8,128)}) custom-call(f32[2,64,128]{2,1,0:T(8,128)} %get-tuple-element.31.o_ref, f32[2,16,128]{2,1,0:T(8,128)} %copy-done.1, f32[2,16,128]{2,1,0:T(8,128)} %copy-done.2), custom_call_target="tpu_custom_call" | custom-call | tf_op jit(solution)/shard_map/yslab/pallas_call | solution.py:24
  28.0 5.3 %collective-permute-start.2 = (f32[2,24,128]{2,1,0:T(8,128)}, f32[2,24,128]{2,1,0:T(8,128)S(1)}, u32[]{:S(2)}, u32[]{:S(2)}) collective-permute-start(f32[2,24,128]{2,1,0:T(8,128)} %get-tuple-element.34), channel_id=1, source_target_pairs={{0,4},{4,8},{8,12},{12,16},{16,20},{20,24},{24,28},{28,0},{1,5},{5... | collective-permute-start | bytes 73736 | tf_op jit(solution)/shard_map/ppermute | solution.py:432
  33.3 14.0 %collective-permute-start.3 = (f32[2,24,128]{2,1,0:T(8,128)}, f32[2,24,128]{2,1,0:T(8,128)S(1)}, u32[]{:S(2)}, u32[]{:S(2)}) collective-permute-start(f32[2,24,128]{2,1,0:T(8,128)} %get-tuple-element.35), channel_id=1, source_target_pairs={{0,28},{4,0},{8,4},{12,8},{16,12},{20,16},{24,20},{28,24},{1,29},{... | collective-permute-start | bytes 73736 | tf_op jit(solution)/shard_map/ppermute | solution.py:432
  48.0 0.6 tile.22.ce_ref
  48.6 0.6 tile.25.ct_ref
  49.3 0.6 broadcast.9
  49.8 0.7 reduce.3
  50.7 0.7 reshape.33.nb_ref
  51.4 0.8 copy.18.wo
  52.1 1.4 %index.1 = (bf16[144,640]{1,0:T(8,128)(2,1)}, f32[8,640]{1,0:T(8,128)}) custom-call(s32[1]{0:T(128)} %bitcast.8.alive_ref, s32[1,512]{1,0:T(1,128)} %reshape.33.nb_ref, s32[1,128]{1,0:T(1,128)} %tile.22.ce_ref, s32[1,128]{1,0:T(1,128)} %tile.25.ct_ref), custom_call_target="tpu_custom_call" | custom-call | tf_op jit(solution)/shard_map/index/pallas_call | solution.py:24
  53.5 1.8 %weights.1 = (bf16[64,48]{1,0:T(8,128)(2,1)}, bf16[64,192]{1,0:T(8,128)(2,1)}, bf16[64,192]{1,0:T(8,128)(2,1)}, bf16[64,768]{1,0:T(8,128)(2,1)}, bf16[256,192]{1...) custom-call(f32[12,64]{1,0:T(8,128)} %w2.1, ...), custom_call_target="tpu_custom_call" | custom-call | tf_op jit(solution)/shard_map/weights/pallas_call | solution.py:24
  55.4 0.6 copy-done.3
  56.0 5.2 %pairs.1 = (f32[1,1,16]{2,1,0:T(1,128)}, f32[2,64,128]{2,1,0:T(8,128)}, f32[2,16,128]{2,1,0:T(8,128)}, f32[2,16,128]{2,1,0:T(8,128)}, f32[2,24,128]{2,1,0:T(8,128)}, /*index=5*/f32[2,24,128]{2,1,0:T(8,128)}) custom-call(bf16[144,640]{1,0:T(8,128)(2,1)} %get-tuple-element.29.oh_ref, f32[8,640]{1,0:T(8,128)} %get-tuple-element.30.geo_ref, ...), custom_call_target="tpu_custom_call" | custom-call | tf_op jit(solution)/shard_map/pairs/pallas_call | solution.py:24
  61.2 1.9 %collective-permute-start.4 = (f32[2,24,128]{2,1,0:T(8,128)}, f32[2,24,128]{2,1,0:T(8,128)S(1)}, u32[]{:S(2)}, u32[]{:S(2)}) collective-permute-start(f32[2,24,128]{2,1,0:T(8,128)} %get-tuple-element.49), channel_id=1, source_target_pairs={{0,4},{4,8},{8,12},{12,16},{16,20},{20,24},{24,28},{28,0},{1,5},{5... | collective-permute-start | bytes 73736 | tf_op jit(solution)/shard_map/ppermute | solution.py:432
  63.2 5.1 %collective-permute-start.5 = (f32[2,24,128]{2,1,0:T(8,128)}, f32[2,24,128]{2,1,0:T(8,128)S(1)}, u32[]{:S(2)}, u32[]{:S(2)}) collective-permute-start(f32[2,24,128]{2,1,0:T(8,128)} %get-tuple-element.50), channel_id=1, source_target_pairs={{0,28},{4,0},{8,4},{12,8},{16,12},{20,16},{24,20},{28,24},{1,29},{... | collective-permute-start | bytes 73736 | tf_op jit(solution)/shard_map/ppermute | solution.py:432
  68.4 1.6 %collective-permute-done.5.hi = f32[2,24,128]{2,1,0:T(8,128)S(1)} collective-permute-done((f32[2,24,128]{2,1,0:T(8,128)}, f32[2,24,128]{2,1,0:T(8,128)S(1)}, u32[]{:S(2)}, u32[]{:S(2)}) %collective-permute-start.5) | collective-permute-done | bytes 24608 | tf_op jit(solution)/shard_map/ppermute | solution.py:432
  70.0 0.6 copy-done.6
  70.6 1.5 %yfold.1 = (f32[2,64,128]{2,1,0:T(8,128)}, f32[2,16,128]{2,1,0:T(8,128)}, f32[2,16,128]{2,1,0:T(8,128)}) custom-call(f32[2,64,128]{2,1,0:T(8,128)} %get-tuple-element.46.fo, f32[2,16,128]{2,1,0:T(8,128)} %get-tuple-element.47.fm, f32[2,16,128]{2,1,0:T(8,128)} %get-tuple-element.48.fp, f32[2,24,128]{2,1,0:T(8,128)} %copy-done.5, f32[2,24,128]{2,1,0:T(8,128)} %copy-done.6), custom_call_target="tpu_custom_call" | custom-call | tf_op jit(solution)/shard_map/yfold/pallas_call | solution.py:24
  72.1 1.9 %collective-permute-start.6 = (f32[2,16,128]{2,1,0:T(8,128)}, f32[2,16,128]{2,1,0:T(8,128)S(1)}, u32[]{:S(2)}, u32[]{:S(2)}) collective-permute-start(f32[2,16,128]{2,1,0:T(8,128)} %get-tuple-element.52), channel_id=1, source_target_pairs={{0,32},{32,64},{64,96},{96,128},{128,160},{160,192},{192,224},{224... | collective-permute-start | bytes 49160 | tf_op jit(solution)/shard_map/ppermute | solution.py:432
  74.0 3.9 %collective-permute-start.7 = (f32[2,16,128]{2,1,0:T(8,128)}, f32[2,16,128]{2,1,0:T(8,128)S(1)}, u32[]{:S(2)}, u32[]{:S(2)}) collective-permute-start(f32[2,16,128]{2,1,0:T(8,128)} %get-tuple-element.53), channel_id=1, source_target_pairs={{0,992},{32,0},{64,32},{96,64},{128,96},{160,128},{192,160},{224,1... | collective-permute-start | bytes 49160 | tf_op jit(solution)/shard_map/ppermute | solution.py:432
  78.0 6.1 %collective-permute-done.7.hi = f32[2,16,128]{2,1,0:T(8,128)S(1)} collective-permute-done((f32[2,16,128]{2,1,0:T(8,128)}, f32[2,16,128]{2,1,0:T(8,128)S(1)}, u32[]{:S(2)}, u32[]{:S(2)}) %collective-permute-start.7) | collective-permute-done | bytes 16416 | tf_op jit(solution)/shard_map/ppermute | solution.py:432
  84.1 0.6 copy-done.8
  84.7 1.6 %xfold.1 = (f32[64,128]{1,0:T(8,128)}, f32[64,128]{1,0:T(8,128)}) custom-call(f32[2,64,128]{2,1,0:T(8,128)} %get-tuple-element.51.fo, f32[2,16,128]{2,1,0:T(8,128)} %copy-done.7, f32[2,16,128]{2,1,0:T(8,128)} %copy-done.8), custom_call_target="tpu_custom_call" | custom-call | tf_op jit(solution)/shard_map/xfold/pallas_call | solution.py:24
  86.3 6.6 %all-gather.1 = f32[256,128]{1,0:T(8,128)} all-gather(f32[64,128]{1,0:T(8,128)} %get-tuple-element.55), channel_id=3, replica_groups=mesh['gx'=32,'gy'=8,'gz'=4] {'gz'}, dimensions={0}, use_global_device_ids=true | all-gather | bytes 163840 | tf_op jit(solution)/shard_map/all_gather | solution.py:504
  92.9 1.8 %zfold.1 = f32[1,1,4608]{2,1,0:T(1,128)} custom-call(s32[1]{0:T(128)} %bitcast.4.e_ref, f32[64,128]{1,0:T(8,128)} %get-tuple-element.54.f_ref, f32[4,64,128]{2,1,0:T(8,128)} %bitcast.9, bf16[128,128]{1,0:T(8,128)(2,1)} %constant.9.clone.p_ref), custom_call_target="tpu_custom_call" | custom-call | tf_op jit(solution)/shard_map/zfold/pallas_call | solution.py:24
  (29 shorter events, 0.3 us)
Async XLA Ops:
  10.9 6.8 %collective-permute-start = (f32[2,16,128]{2,1,0:T(8,128)}, f32[2,16,128]{2,1,0:T(8,128)S(1)}, u32[]{:S(2)}, u32[]{:S(2)}) collective-permute-start(f32[2,16,128]{2,1,0:T(8,128)} %get-tuple-element.32), channel_id=1, source_target_pairs={{0,32},{32,64},{64,96},{96,128},{128,160},{160,192},{192,224},{224... | collective-permute-start | bytes 49160 | tf_op jit(solution)/shard_map/ppermute | solution.py:432
  15.8 10.1 %collective-permute-start.1 = (f32[2,16,128]{2,1,0:T(8,128)}, f32[2,16,128]{2,1,0:T(8,128)S(1)}, u32[]{:S(2)}, u32[]{:S(2)}) collective-permute-start(f32[2,16,128]{2,1,0:T(8,128)} %get-tuple-element.33), channel_id=1, source_target_pairs={{0,992},{32,0},{64,32},{96,64},{128,96},{160,128},{192,160},{224,1... | collective-permute-start | bytes 49160 | tf_op jit(solution)/shard_map/ppermute | solution.py:432
  17.7 8.1 %copy-start.1 = (f32[2,16,128]{2,1,0:T(8,128)}, f32[2,16,128]{2,1,0:T(8,128)S(1)}, u32[]{:S(2)}) copy-start(f32[2,16,128]{2,1,0:T(8,128)S(1)} %collective-permute-done.m_ref.xm_ref) | copy-start | bytes 49156
  25.8 0.6 copy-start.2
  26.4 21.6 %copy-start.10 = (s32[1,1,16]{2,1,0:T(1,128)S(1)}, s32[1,1,16]{2,1,0:T(1,128)}, u32[]{:S(2)}) copy-start(s32[1,1,16]{2,1,0:T(1,128)} %param.15) | copy-start | bytes 196
  26.4 22.2 %copy-start.11 = (s32[1,1,16]{2,1,0:T(1,128)S(1)}, s32[1,1,16]{2,1,0:T(1,128)}, u32[]{:S(2)}) copy-start(s32[1,1,16]{2,1,0:T(1,128)} %param.17) | copy-start | bytes 196
  26.4 23.4 %copy-start.9 = (s32[1,1,512]{2,1,0:T(1,128)S(1)}, s32[1,1,512]{2,1,0:T(1,128)}, u32[]{:S(2)}) copy-start(s32[1,1,512]{2,1,0:T(1,128)} %param.16) | copy-start | bytes 6148
  28.0 23.4 %copy-start = (f32[256,64]{0,1:T(8,128)S(1)}, f32[256,64]{0,1:T(8,128)}, u32[]{:S(2)}) copy-start(f32[256,64]{0,1:T(8,128)} %param.22) | copy-start | bytes 196612
  28.0 27.4 %collective-permute-start.2 = (f32[2,24,128]{2,1,0:T(8,128)}, f32[2,24,128]{2,1,0:T(8,128)S(1)}, u32[]{:S(2)}, u32[]{:S(2)}) collective-permute-start(f32[2,24,128]{2,1,0:T(8,128)} %get-tuple-element.34), channel_id=1, source_target_pairs={{0,4},{4,8},{8,12},{12,16},{16,20},{20,24},{24,28},{28,0},{1,5},{5... | collective-permute-start | bytes 73736 | tf_op jit(solution)/shard_map/ppermute | solution.py:432
  33.3 22.1 %collective-permute-start.3 = (f32[2,24,128]{2,1,0:T(8,128)}, f32[2,24,128]{2,1,0:T(8,128)S(1)}, u32[]{:S(2)}, u32[]{:S(2)}) collective-permute-start(f32[2,24,128]{2,1,0:T(8,128)} %get-tuple-element.35), channel_id=1, source_target_pairs={{0,28},{4,0},{8,4},{12,8},{16,12},{20,16},{24,20},{28,24},{1,29},{... | collective-permute-start | bytes 73736 | tf_op jit(solution)/shard_map/ppermute | solution.py:432
  55.4 0.6 copy-start.3
  55.4 0.6 copy-start.4
  61.2 7.1 %collective-permute-start.4 = (f32[2,24,128]{2,1,0:T(8,128)}, f32[2,24,128]{2,1,0:T(8,128)S(1)}, u32[]{:S(2)}, u32[]{:S(2)}) collective-permute-start(f32[2,24,128]{2,1,0:T(8,128)} %get-tuple-element.49), channel_id=1, source_target_pairs={{0,4},{4,8},{8,12},{12,16},{16,20},{20,24},{24,28},{28,0},{1,5},{5... | collective-permute-start | bytes 73736 | tf_op jit(solution)/shard_map/ppermute | solution.py:432
  63.2 6.8 %collective-permute-start.5 = (f32[2,24,128]{2,1,0:T(8,128)}, f32[2,24,128]{2,1,0:T(8,128)S(1)}, u32[]{:S(2)}, u32[]{:S(2)}) collective-permute-start(f32[2,24,128]{2,1,0:T(8,128)} %get-tuple-element.50), channel_id=1, source_target_pairs={{0,28},{4,0},{8,4},{12,8},{16,12},{20,16},{24,20},{28,24},{1,29},{... | collective-permute-start | bytes 73736 | tf_op jit(solution)/shard_map/ppermute | solution.py:432
  68.4 1.6 %copy-start.5 = (f32[2,24,128]{2,1,0:T(8,128)}, f32[2,24,128]{2,1,0:T(8,128)S(1)}, u32[]{:S(2)}) copy-start(f32[2,24,128]{2,1,0:T(8,128)S(1)} %collective-permute-done.4.lo) | copy-start | bytes 73732
  70.0 0.6 copy-start.6
  72.1 5.8 %collective-permute-start.6 = (f32[2,16,128]{2,1,0:T(8,128)}, f32[2,16,128]{2,1,0:T(8,128)S(1)}, u32[]{:S(2)}, u32[]{:S(2)}) collective-permute-start(f32[2,16,128]{2,1,0:T(8,128)} %get-tuple-element.52), channel_id=1, source_target_pairs={{0,32},{32,64},{64,96},{96,128},{128,160},{160,192},{192,224},{224... | collective-permute-start | bytes 49160 | tf_op jit(solution)/shard_map/ppermute | solution.py:432
  74.0 10.1 %collective-permute-start.7 = (f32[2,16,128]{2,1,0:T(8,128)}, f32[2,16,128]{2,1,0:T(8,128)S(1)}, u32[]{:S(2)}, u32[]{:S(2)}) collective-permute-start(f32[2,16,128]{2,1,0:T(8,128)} %get-tuple-element.53), channel_id=1, source_target_pairs={{0,992},{32,0},{64,32},{96,64},{128,96},{160,128},{192,160},{224,1... | collective-permute-start | bytes 49160 | tf_op jit(solution)/shard_map/ppermute | solution.py:432
  78.0 6.1 %copy-start.7 = (f32[2,16,128]{2,1,0:T(8,128)}, f32[2,16,128]{2,1,0:T(8,128)S(1)}, u32[]{:S(2)}) copy-start(f32[2,16,128]{2,1,0:T(8,128)S(1)} %collective-permute-done.6.lo) | copy-start | bytes 49156
  84.1 0.6 copy-start.8
